TPU v7x, 128 devices: a whole 4x4x4 slice. The times are simulated.
128 devices in a mesh: rep: 2 (over core), dp: 64 (over x, y, z).
Axes of the slice: x: 4, y: 4, z: 4, core: 2. Of those that a mesh axis runs over, the one named last changes fastest.
Arguments:
- x: bfloat16 [128, 2048, 1024], P(('rep', 'dp')), parts along dimension 0
- dy: bfloat16 [128, 2048, 1024], P(('rep', 'dp')), parts along dimension 0
- w_gate: bfloat16 [2, 1024, 2560], P(None, 'dp')
- w_up: bfloat16 [2, 1024, 2560], P(None, 'dp')
- w_down: bfloat16 [2, 2560, 1024], P(None, 'dp')
Outputs:
- output 1: bfloat16 [128, 2048, 1024], P(('rep', 'dp')), parts along dimension 0
- output 2: bfloat16 [4, 1024, 2560], P('rep', 'dp'), parts along dimension 0
- output 3: bfloat16 [4, 1024, 2560], P('rep', 'dp'), parts along dimension 0
- output 4: bfloat16 [4, 2560, 1024], P('rep', 'dp'), parts along dimension 0
There are 2 independent parts. A program takes and returns all parts, laid end to end along the dimension named above; an argument that names none is the same for every part.
All inputs are finite; a program needn't handle non-finite values.
Results may differ from a plain program's by a relative error of at most 0.018.
Values are sent between devices in bfloat16 or wider.
A program may use at most 1.5 GiB of HBM per device.

v0:
```python
import jax
import jax.numpy as jnp
from jax import lax
from jax.experimental import pallas as pl
from jax.experimental.pallas import tpu as pltpu
from jax.sharding import PartitionSpec as P

MESH = pl.DeviceIdType.MESH
BF, F32 = jnp.bfloat16, jnp.float32
ANY = pl.BlockSpec(memory_space=pl.ANY)
VM = pl.BlockSpec(memory_space=pltpu.VMEM)
T, D, FF = 2048, 1024, 2560
RING, LANES, ROWS, MXU = 4, 128, 8, 256
PAIR = 2 * ROWS
CUBE = (RING,) * 3
UNITS = 20
HIGH = UNITS * PAIR * LANES // D // ROWS
AXES = range(3)
BOTH = range(2)
STEPS = (1, -1, 2)
SIDES = ((0, 1), (1, -1))
EVERY = slice(None)
TWO = slice(0, 2)
VMEM = 67_043_328

GATHER_ORDERS = ((2, 1, 0), (0, 2, 1), (1, 0, 2))
SCATTER_ORDERS = ((0, 1, 2), (1, 2, 0), (2, 0, 1))
SHARES = ((0, 7), (7, 14), (14, 20))


class Place:
    def __init__(self):
        self.core = lax.axis_index("rep")
        me = lax.axis_index("dp")
        self.at = (me // RING**2, (me // RING) % RING, me % RING)
        self.on = {(a, step): (self.at[a] + (step + RING)) % RING for a in AXES for step in STEPS}

    def along(self, axis, step):
        return self.on[axis, step]

    def peer(self, axis, step):
        x, y, z = (self.along(a, step) if a == axis else self.at[a] for a in AXES)
        return {"dp": (x * RING + y) * RING + z}

    def other(self):
        return {"rep": 1 - self.core}


def enter(place, other):
    barrier = pltpu.get_barrier_semaphore()
    for axis in AXES:
        for step in STEPS:
            pl.semaphore_signal(barrier, inc=1, device_id=place.peer(axis, step), device_id_type=MESH)
    if other:
        pl.semaphore_signal(barrier, inc=1, device_id=place.other(), device_id_type=MESH)
    return lambda: pl.semaphore_wait(barrier, len(STEPS) * len(AXES) + other)


def remote(src, dst, send, recv, device):
    return pltpu.make_async_remote_copy(src_ref=src, dst_ref=dst, send_sem=send, recv_sem=recv, device_id=device, device_id_type=MESH)


def wait_for(what, sem):
    pltpu.make_async_copy(what, what, sem).wait()


def row_mean(x):
    return jnp.mean(x, -1, keepdims=True)


def norm_scale(wide):
    return lax.rsqrt(row_mean(wide * wide) + 1e-6)


def normed(h):
    wide = h.astype(F32)
    return (wide * norm_scale(wide)).astype(BF)


def dot(a, b, over_a=1, over_b=0):
    return lax.dot_general(a, b, (((over_a,), (over_b,)), ((), ())), preferred_element_type=F32)


def at_step(hooks, step):
    for number, hook in hooks.items():
        pl.when(step == number)(hook)


class Gather:
    def __init__(self, name, place, full, parts, send, recv):
        self.name, self.p, self.full, self.parts, self.send, self.recv = name, place, full, parts, send, recv

    STARTS = (0, 3, 5, 7, 10, 14, 16)
    CROSS = (9, 12, 13, 14, 15)

    def view(self, color, where):
        at = [where.get(a, self.p.at[a]) for a in AXES]
        return self.full.at[(*at, *self.parts[color])]

    def copy(self, color, slot):
        a, b, c = GATHER_ORDERS[color]
        p = self.p
        stage = sum(slot >= first for first in self.STARTS) - 1
        group = len(self.CROSS) if slot in self.CROSS else stage
        sems = self.send.at[color, group], self.recv.at[color, group]
        k = slot - self.STARTS[stage]
        if stage == 0:
            block = self.view(color, {})
            return remote(block, block, *sems, p.peer(a, STEPS[k]))
        axis, done, split = (b, {a: EVERY}, a) if stage < 3 else (c, {a: EVERY, b: EVERY}, b)
        side = k % 2
        step, half = STEPS[side], slice(2 * side, 2 * side + 2)
        where = dict(done)
        if stage in (2, 4):
            where[axis] = p.along(axis, -step)
            if slot not in self.CROSS:
                where[split] = half
        if stage == 5:
            where.update({axis: p.along(axis, 2), split: half})
        block = self.view(color, where)
        return remote(block, block, *sems, p.other() if slot in self.CROSS else p.peer(axis, step))

    def wait(self, color, group, sems):
        a, b, c = GATHER_ORDERS[color]
        ab = {a: EVERY, b: EVERY}
        where = {a: slice(len(STEPS))}, {a: EVERY, b: TWO}, {a: EVERY}, {**ab, c: TWO}, ab, {**ab, c: EVERY}
        wait_for(self.view(color, where[group]), sems.at[color, group])

    def stage(self, number):
        last = len(self.STARTS) - 1
        for color in AXES:
            if number:
                self.wait(color, number - 1, self.recv)
            for slot in range(self.STARTS[number], self.STARTS[number + 1]) if number < last else ():
                self.copy(color, slot).start()
            if 0 < number < last:
                self.wait(color, number - 1, self.send)

    def finish(self):
        for color in AXES:
            self.wait(color, len(self.CROSS), self.send)


def gather_parts(core):
    columns = []
    for layer in (((3, 3, 2), (2, 2, 2), (2, 2, 2)), ((4, 3, 3), (3, 4, 3))):
        first = 0
        columns.append([])
        for widths in layer:
            columns[-1].append([])
            for width in widths:
                columns[-1][-1].append((EVERY, slice(first * LANES, (first + width) * LANES)))
                first += width
    half = part(core, D // 2)
    return columns, [(slice(*cut), EVERY, half) for cut in ((4, 5), (0, 2), (2, 4))]


def slots(*groups):
    def hook():
        for job, stage in groups:
            with jax.named_scope(f"{job.name}_{stage}"):
                job.stage(stage)

    return hook


def spread(jobs, table, sizes):
    plan = {}
    for n, (job, steps) in enumerate(zip(jobs, table, strict=True)):
        for stage, step in enumerate(steps):
            plan.setdefault(step, []).append((-stage, n, job))
    hooks, first = [], 0
    for size in sizes:
        steps = [step for step in sorted(plan) if first <= step < first + size]
        hooks.append({step - first: slots(*((job, -late) for late, _, job in sorted(plan[step], key=lambda t: t[:2]))) for step in steps})
        first += size
    return hooks


class Scatter:
    STARTS = (0, 2, 4, 6, 8, 11)

    def __init__(self, place, mine, put, number, bufs, send, recv, recv_c):
        self.name = f"rs{number}"
        self.p, self.mine, self.put, self.number, self.send, self.recv, self.recv_c = place, mine, put, number, send, recv, recv_c
        self.in_a, self.in_h, self.acc_b, self.send_b, self.in_b, self.in_bh, self.acc_c, self.send_c, self.in_c = bufs

    def sems(self, color, stage):
        twin = self.number % 2
        return self.send.at[twin, color, stage], self.recv.at[twin, color, stage] if stage < 4 else self.recv_c.at[self.number, color]

    def arrived(self, color, stage):
        twin = self.number % 2
        what = (self.in_h[color].at[twin], self.in_a[color].at[twin], self.in_bh[color], self.in_b[color], self.in_c[color].at[self.number])
        wait_for(what[stage], self.sems(color, stage)[1])

    def sent(self, color, stage):
        mine = lambda where: self.mine.at[self.term(color, (where, EVERY, EVERY))]
        send_b = self.send_b[color]
        what = (mine(0), mine(TWO), send_b.at[0], send_b.at[TWO], self.send_c[color].at[slice(len(STEPS))])
        wait_for(what[stage], self.sems(color, stage)[0])

    def term(self, color, where):
        at = dict(zip(SCATTER_ORDERS[color], where))
        return (*(at[axis] for axis in AXES), slice(*SHARES[color]))

    def copy(self, color, slot):
        a, b, c = SCATTER_ORDERS[color]
        p = self.p
        twin = self.number % 2
        stage = sum(slot >= first for first in self.STARTS) - 1
        k = slot - self.STARTS[stage]
        sems = self.sems(color, stage)
        step, half = STEPS[k], pl.ds(2 * k, 2)
        if stage == 0:
            src, dst, axis = self.mine.at[self.term(color, (p.along(a, 2), half, EVERY))], self.in_h[color].at[twin, k], a
        elif stage == 1:
            src, dst, axis = self.mine.at[self.term(color, (p.along(a, step), EVERY, EVERY))], self.in_a[color].at[twin, k], a
        elif stage == 2:
            src, dst, axis = self.send_b[color].at[p.along(b, 2), half], self.in_bh[color].at[k], b
        elif stage == 3:
            src, dst, axis = self.send_b[color].at[p.along(b, step)], self.in_b[color].at[k], b
        else:
            src, dst, axis = self.send_c[color].at[p.along(c, step)], self.in_c[color].at[self.number, k], c
        return remote(src, dst, *sems, p.peer(axis, step))

    def stage(self, number):
        last = len(self.STARTS) - 1
        for color, axes in enumerate(SCATTER_ORDERS):
            if number:
                self.arrived(color, number - 1)
            self.sum(number, color, *axes)
            for slot in range(self.STARTS[number], self.STARTS[number + 1]) if number < last else ():
                self.copy(color, slot).start()
            for stage in range(2 * (number - 3), min(2 * number - 4, last)) if number > 2 else ():
                self.sent(color, stage)

    def sum(self, number, color, a, b, c):
        p, mine, twin = self.p, self.mine, self.number % 2
        in_a, in_h, acc_b, send_b, in_b, in_bh = (
            t[color] for t in (self.in_a, self.in_h, self.acc_b, self.send_b, self.in_b, self.in_bh)
        )
        acc_c, send_c, in_c = (t[color] for t in (self.acc_c, self.send_c, self.in_c))
        flip = (lambda i, j: (i, j)) if b < c else (lambda i, j: (j, i))
        if number == 1:
            for slot, step in SIDES:

                @pl.loop(0, 2 * RING, unroll=2)
                def _(k):
                    i, j = k // RING, k % RING
                    at = self.term(color, (p.along(a, step), 2 * slot + i, j))
                    mine[at] = (mine[at].astype(F32) + in_h[(twin, slot, *flip(i, j))].astype(F32)).astype(BF)

        if number == 2:

            @pl.loop(0, RING**2, unroll=2)
            def _(k):
                i, j = k // RING, k % RING
                total = mine[self.term(color, (p.at[a], i, j))].astype(F32)
                for slot, _ in SIDES:
                    total = total + in_a[(twin, slot, *flip(i, j))].astype(F32)
                acc_b[i, j] = total
                send_b[i, j] = total.astype(BF)

        if number == 3:
            for slot, step in SIDES:
                i = p.along(b, step)

                @pl.loop(0, 2)
                def _(j):
                    send_b[i, 2 * slot + j] = (acc_b[i, 2 * slot + j] + in_bh[slot, j].astype(F32)).astype(BF)

        if number == 4:

            @pl.loop(0, RING)
            def _(j):
                total = acc_b[p.at[b], j]
                for slot, _ in SIDES:
                    total = total + in_b[slot, j].astype(F32)
                acc_c[j] = total
                send_c[j] = total.astype(BF)

        if number == 5:
            total = acc_c[p.at[c]]
            for slot in AXES:
                total = total + in_c[self.number, slot].astype(F32)
            lo, hi = SHARES[color]
            for k in range(lo, hi):
                self.put(k, total[k - lo])


def scatter_scratch(jobs):
    two, ring = (2,), (RING,)
    groups = []
    for (lo, hi), (a, b, c) in zip(SHARES, SCATTER_ORDERS):
        half = two + ring if b < c else ring + two
        shapes = (
            (two + two + ring + ring, BF), (two + two + half, BF), (ring + ring, F32), (ring + ring, BF), (two + ring, BF), (two + two, BF),
            (ring, F32), (ring, BF), ((jobs, len(STEPS)), BF),
        )
        groups.append([pltpu.VMEM((*shape, hi - lo, PAIR, LANES), kind) for shape, kind in shapes])
    return zip(*groups)


def put_gate_up(out):
    def put(k, unit):
        out[:, part(k, LANES)] = unit.astype(BF)

    return put


def put_half(outs, half):
    def put(k, unit):
        which, col = k // (UNITS // 2), k % (UNITS // 2) + half * (UNITS // 2)
        outs[which][:, part(col, LANES)] = unit.astype(BF)

    return put


def put_down(out):
    def put(k, unit):
        extra = k - D // LANES * 2
        if extra < 0:
            out[part(k % 2, PAIR), part(k // 2, LANES)] = unit.astype(BF)
        else:
            for n in BOTH:
                out[part(HIGH - 1, ROWS), part(2 * extra + n, LANES)] = unit[ROWS * n : ROWS * (n + 1)].astype(BF)

    return put


def part(k, size):
    return slice(k * size, (k + 1) * size) if isinstance(k, int) else pl.ds(pl.multiple_of(k * size, size), size)


def blocks(shape, places, **mode):
    return pl.BlockSpec(shape, lambda *at: tuple(at[places[k]] if k in places else 0 for k in range(len(shape))), **mode)


def silu_parts(gate):
    s = jax.nn.sigmoid(gate)
    silu = gate * s
    return silu, s + silu * (1 - s)


FORWARD_STEPS = (9, FF // MXU, 4, 8)
GATHERS = (
    (0, 1, 2, 3, 5, 7, 8),
    (0, 1, 2, 5, 10, 12, 13),
    (0, 1, 2, 7, 12, 15, 16),
    (0, 4, 6, 11, 15, 18, 19),
    (0, 4, 6, 15, 19, 21, 23),
    (0, 4, 6, 13, 17, 20, 23),
    (0, 4, 6, 18, 21, 23, 25),
)


def forward_kernel(
    g_ref, u_ref, d_ref, x_ref, dy_ref, gu_out, d_out, aT0, ways, act1, h1, aT1, act2, dgu2, gu_v, d_v, a_v, h_v, t_v, dy_v, sem, send, recv
):
    place = Place()
    core = place.core
    sems = [sem.at[k] for k in range(sem.shape[0])]

    def copy(src, dst):
        at = sems.pop()
        made = lambda: pltpu.make_async_copy(src, dst, at)
        return lambda: made().start(), lambda: made().wait()

    fetch_x, fetch_dy = copy(x_ref, h_v), copy(dy_ref, dy_v)
    puts = [copy(t_v, aT0), copy(t_v, aT1), copy(gu_v.at[0], gu_out.at[0]), copy(gu_v.at[1], gu_out.at[1]), copy(d_v.at[0], d_out)]
    put_t0, put_t1, *put_w = puts
    fetch_x[0]()
    columns, rows_of_down = gather_parts(core)
    half = rows_of_down[0][-1]
    for n in range(g_ref.shape[0]):
        gu_v[(n, core, *place.at)] = jnp.where(core == 0, g_ref[n], u_ref[n])
        d_v[(n, *place.at, EVERY, EVERY, half)] = d_ref[n, :, :, half]
    entered = enter(place, 1)
    fetch_dy[0]()
    plan = [(gu_v.at[0, core], piece) for piece in columns[0]]
    early, late = columns[1]
    plan += [(d_v.at[0], rows_of_down), (gu_v.at[1, core], early), (d_v.at[1], rows_of_down), (gu_v.at[1, core], late)]
    jobs = [Gather(f"ag{n}", place, *what, send.at[n], recv.at[n]) for n, what in enumerate(plan)]
    prelude, *hooks = spread(jobs, GATHERS, FORWARD_STEPS)
    with jax.named_scope("enter"):
        entered()

    def norm_rows(k):
        rows = part(k, MXU)
        a = normed(h_v[rows])
        a_v[rows] = a
        t_v[:, rows] = a.T

    for step in sorted(prelude):
        prelude[step]()
        if step == 0:
            fetch_x[1]()
        if step < 2:
            with jax.named_scope("norm"):
                pl.loop(RING * step, RING * (step + 1))(norm_rows)
    put_t0[0]()

    def gate_up_body(out_ways, out_act):
        step = pl.program_id(0)
        at_step(hooks[0], step)
        w = [gu_v[0, m, :, :, :, :, part(step, MXU)].reshape(D, MXU) for m in BOTH]
        tall = T // RING
        for k in range(RING):
            rows = part(k, tall)
            gate, up = (dot(a_v[rows], w[m]) for m in BOTH)
            silu, slope = silu_parts(gate)
            for m, val in enumerate((up * slope, silu)):
                out_ways[m, rows] = val
            out_act[rows] = (silu * up).astype(BF)

    with jax.named_scope("P1"):
        outs = [blocks((2, T, MXU), {2: 0}), blocks((T, MXU), {1: 0})]
        pltpu.emit_pipeline(gate_up_body, grid=(FF // MXU,), out_specs=outs)(ways, act1)
    put_t0[1]()

    wide = 512

    def down_body(act, out_h):
        step = pl.program_id(0)
        at_step(hooks[1], step)
        for k in range(wide // MXU):
            rows = part(k, MXU)
            there = part(step * (wide // MXU) + k, MXU)
            out = dot(act[rows], d_v[0].reshape(FF, D)).astype(BF)
            h = (h_v[there].astype(F32) + out.astype(F32)).astype(BF)
            out_h[rows] = h
            a = normed(h)
            a_v[there] = a
            t_v[:, there] = a.T

    with jax.named_scope("P2"):
        pltpu.emit_pipeline(
            down_body, grid=(T // wide,), in_specs=[blocks((wide, FF), {0: 0})], out_specs=[blocks((wide, D), {0: 0})]
        )(act1, h1)
    put_t1[0]()
    fetch_dy[1]()

    def finish():
        for job in jobs:
            job.finish()

    last = hooks[2]
    for step, start in enumerate((*(put[0] for put in put_w), finish), 3):
        last[step] = start

    def second_body(out_act, out_dgu):
        col, row = pl.program_id(0), pl.program_id(1)
        at_step(last, col * (T // wide) + row)
        rows = part(row, wide)
        a, dy = a_v[rows], dy_v[rows]
        wd = d_v[1, pl.ds(2 * col, 2)].reshape(FF // 2 // ROWS, ROWS, D)
        for k in range(FF // 2 // MXU):
            cols = part(k, MXU)
            there = part(col * (FF // 2 // MXU) + k, MXU)
            gate, up = (dot(a, gu_v[1, m, :, :, :, :, there].reshape(D, MXU)) for m in BOTH)
            by_act = dot(dy, wd[part(k, MXU // ROWS)].reshape(MXU, D), 1, 1).astype(BF).astype(F32)
            silu, slope = silu_parts(gate)
            out_act[:, cols] = (silu * up).astype(BF)
            for m, val in enumerate((by_act * up * slope, by_act * silu)):
                out_dgu[m, :, cols] = val.astype(BF)

    with jax.named_scope("P3"):
        outs = [blocks((wide, FF // 2), {0: 1, 1: 0}), blocks((2, wide, FF // 2), {1: 1, 2: 0})]
        pltpu.emit_pipeline(second_body, grid=(2, T // wide), out_specs=outs)(act2, dgu2)
    with jax.named_scope("puts"):
        for put in (put_t1, *put_w):
            put[1]()


def shaped(*shape, kind=BF):
    return jax.ShapeDtypeStruct(shape, kind)


def calls(kernel, number, ins, outs, scratch):
    return pl.pallas_call(
        kernel,
        out_shape=tuple(shape for shape, _ in outs),
        in_specs=ins,
        out_specs=tuple(spec for _, spec in outs),
        scratch_shapes=scratch,
        compiler_params=pltpu.CompilerParams(collective_id=number, has_side_effects=True, vmem_limit_bytes=VMEM),
        name=kernel.__name__,
    )


def forward(wg, wu, wd, x, dy):
    layers, rows = wg.shape[:-1]
    outs = [
        shaped(layers, 2, *CUBE, rows, FF), shaped(*CUBE, HIGH, ROWS, D), shaped(D, T), shaped(2, T, FF, kind=F32), shaped(T, FF),
        shaped(T, D), shaped(D, T), shaped(T, FF), shaped(2, T, FF),
    ]
    scratch = [(layers, 2, *CUBE, rows, FF), (layers, *CUBE, HIGH, ROWS, D), (T, D), (T, D), (D, T), (T, D)]
    sems = [(len(GATHERS),)] + [(len(GATHERS), len(SHARES), 6)] * 2
    scratch = [pltpu.VMEM(t, BF) for t in scratch] + [pltpu.SemaphoreType.DMA(t) for t in sems]
    call = calls(forward_kernel, 0, [VM] * 3 + [ANY] * 2, [(t, ANY) for t in outs], scratch)
    return call(wg, wu, wd.reshape(layers, HIGH, ROWS, D), x, dy)


def down_grad(act, by_out, mine, hooks):
    def body(act_cols):
        k = pl.program_id(0)
        at_step(hooks, k)
        val = dot(act_cols[...], by_out[...], 0, 0)
        tiles = D // LANES
        left = None
        for c in range(tiles):
            col = val[:, part(c, LANES)].reshape(RING**2, HIGH, ROWS, LANES)
            mine[k, :, :, 2 * c : 2 * c + 2] = col[:, : HIGH - 1].reshape(RING, RING, 2, PAIR, LANES).astype(BF)
            last = col[:, HIGH - 1 :]
            if c % 2:
                both = jnp.concatenate([left, last], 1).reshape(RING, RING, PAIR, LANES)
                mine[k, :, :, 2 * tiles + c // 2] = both.astype(BF)
            left = last

    pltpu.emit_pipeline(body, grid=(RING,), in_specs=[blocks((T, FF // RING), {1: 0})])(act)


def gate_up_grads(a_t, dgu, mine, hooks):
    wide = 512
    each = FF // wide

    def body(cols):
        k = pl.program_id(0)
        at_step(hooks, k)
        for n in range(wide // MXU):
            val = dot(a_t[...], cols[:, part(n, MXU)])
            for c in range(MXU // LANES):
                col = val[:, part(c, LANES)].reshape(*CUBE, PAIR, LANES).astype(BF)
                mine[1 + k // each, :, :, :, (k % each) * (wide // LANES) + n * (MXU // LANES) + c] = col

    pltpu.emit_pipeline(body, grid=(2 * each,), in_specs=[pl.BlockSpec((None, T, wide), lambda k: (k // each, 0, k % each))])(dgu)


def state_grad(dgu, w, h, by_out, held, out, keep, hooks):
    steps = T // MXU

    def project(d, k, n):
        cols = part(n, MXU)
        by_gate, by_up = (dot(d[m], w[m, cols], 1, 1).astype(BF).astype(F32) for m in BOTH)
        held[part(k % 2, MXU), cols] = (by_gate + by_up).astype(BF)

    def finish(h, outs, k, n):
        rows = part(n, MXU // RING)
        there = part(jnp.maximum(k - 1, 0) * RING + n, MXU // RING)
        by_a = held[part((k + 1) % 2 * RING + n, MXU // RING), :D].astype(F32)
        wide = h[rows].astype(F32)
        scale = norm_scale(wide)
        inner = row_mean(by_a * wide)
        by_norm = (by_a * scale - wide * (inner * scale * scale * scale)).astype(BF)
        total = (by_out[there].astype(F32) + by_norm.astype(F32)).astype(BF)
        if keep is None:
            outs[0][rows] = total
        else:
            keep[there] = total

    def body(d, h, *outs):
        k = pl.program_id(0)
        at_step(hooks, k)

        @pl.when(k < steps)
        def _():
            for n in range(RING):
                finish(h, outs, k, n)
                project(d, k, n)

        @pl.when(k == steps)
        def _():
            for n in range(RING):
                finish(h, outs, k, n)

    behind = pl.BlockSpec((MXU, D), lambda k: (jnp.maximum(k - 1, 0), 0))
    now = lambda k: jnp.minimum(k, steps - 1)
    if len(dgu.shape) > 3:
        each = steps // 2
        source = pl.BlockSpec((2, None, MXU, FF), lambda k: (0, now(k) // each, now(k) % each, 0))
    else:
        source = pl.BlockSpec((2, MXU, FF), lambda k: (0, now(k), 0))
    pltpu.emit_pipeline(
        body,
        grid=(steps + 1,),
        in_specs=[source, behind],
        out_specs=[behind] if keep is None else [],
    )(dgu, h, *([out] if keep is None else []))


def layer_grads(ways, by_out, w, a_t, mine, held, out, sem, hooks, fetch):
    steps = FF // MXU
    pairs = steps // 2

    def held_at(k, m):
        return part(2 * (k % pairs) + m, MXU)

    def moves(k):
        for m in BOTH:
            for n in BOTH:
                yield pltpu.make_async_copy(held.at[n, :, held_at(k, m)], out.at[m, n, :, part(k, MXU)], sem.at[k % 2, m, n])

    tall = T // 2

    def act(way, k, r):
        rows = part(r, tall)
        by_act = dot(by_out[rows], w[part(k, MXU)], 1, 1).astype(BF).astype(F32)
        for m in BOTH:
            held[r, :, held_at(k, m)] = (by_act * way[m, rows]).astype(BF)

    def weights(k, m):
        val = dot(a_t[...], held[:, :, held_at(k, m)].reshape(T, MXU))
        for c in range(MXU // LANES):
            unit = m * (UNITS // 2) + (k % pairs) * (MXU // LANES) + c
            mine[1 + k // pairs, :, :, :, unit] = val[:, part(c, LANES)].reshape(*CUBE, PAIR, LANES).astype(BF)

    def body(way):
        k = pl.program_id(0)
        at_step(hooks, k)

        @pl.when(k >= 1)
        def _():
            for copy in moves(k - 1):
                copy.start()

        @pl.when(k >= 2)
        def _():
            for copy in moves(k - 2):
                copy.wait()

        @pl.when(k == 0)
        def _():
            for r in BOTH:
                act(way, k, r)

        @pl.when((k > 0) & (k < steps))
        def _():
            for r in BOTH:
                weights(k - 1, r)
                act(way, k, r)

        @pl.when(k == steps)
        def _():
            fetch()
            for r in BOTH:
                weights(k - 1, r)

    block = pl.BlockSpec((2, T, MXU), lambda k: (0, 0, jnp.minimum(k, steps - 1)))
    pltpu.emit_pipeline(body, grid=(steps + 1,), in_specs=[block])(ways)
    for copy in moves(steps - 1):
        copy.wait()


BACKWARD_STEPS = (4, 10, 9, 4, 11, 1, 9, 6)
SCATTERS = (
    (4, 8, 14, 16, 18, 24),
    (9, 16, 21, 24, 26, 29),
    (16, 24, 29, 30, 32, 35),
    (27, 30, 34, 36, 40, 43),
    (33, 35, 40, 42, 46, 48),
    (38, 41, 46, 49, 50, 51),
)


def backward_kernel(
    act2, dy, aT1, dgu2, gu_w, h1, act1, ways, d_w, aT0, x, dx, dgu1, d_out, g_out, u_out, dy_w_v, t_v, dh_v, w_v, mine, *more
):
    *bufs, sem, move_sem, send, recv, recv_c = more
    place = Place()
    sems = [sem.at[k] for k in range(sem.shape[0])]

    def load(src, dst):
        at = sems.pop()
        copy = lambda: pltpu.make_async_copy(src, dst, at)
        return lambda: copy().start(), lambda: copy().wait()

    dy_v = dy_w_v.at[:T]
    early, late = slice(0, FF - 2 * MXU), slice(FF - 2 * MXU, FF)
    loads = [(dy, dy_v), (aT1, t_v), (gu_w.at[1], w_v), (aT0, t_v), (d_w, dy_w_v)]
    loads += [(gu_w.at[0, :, :, cols], w_v.at[:, :, cols]) for cols in (early, late)]
    fetch_dy, fetch_t, fetch_w, fetch_t0, fetch_d, *fetch_w0 = (load(*pair) for pair in loads)
    fetch_dy[0]()
    entered = enter(place, 0)
    groups = [bufs[k : k + len(SHARES)] for k in range(0, len(bufs), len(SHARES))]
    jobs = []
    halves = [put_half((g_out.at[0], u_out.at[0]), half) for half in BOTH]
    for puts in ((put_down(d_out.at[1]), put_gate_up(g_out.at[1]), put_gate_up(u_out.at[1])), (put_down(d_out.at[0]), *halves)):
        for k, put in enumerate(puts):
            n = len(jobs)
            jobs.append(Scatter(place, mine.at[k], put, n, groups, send, recv, recv_c))
    hooks = spread(jobs, SCATTERS, BACKWARD_STEPS)
    for phase, step, fetch in ((0, 1, fetch_t), (1, 2, fetch_w), (3, 2, fetch_t0), (3, 0, fetch_d)):
        hooks[phase][step] = fetch[0]
    fetch_dy[1]()
    with jax.named_scope("P4"):
        down_grad(act2, dy_v, mine.at[0], hooks[0])
    entered()
    fetch_t[1]()
    with jax.named_scope("P5"):
        gate_up_grads(t_v, dgu2, mine, hooks[1])
    fetch_w[1]()
    with jax.named_scope("P6"):
        state_grad(dgu2, w_v, h1, dy_v, t_v, None, dh_v, hooks[2])
    with jax.named_scope("P7"):
        down_grad(act1, dh_v, mine.at[0], hooks[3])
    fetch_d[1]()
    fetch_t0[1]()
    with jax.named_scope("P8"):
        layer_grads(ways, dh_v, dy_w_v, t_v, mine, w_v, dgu1, move_sem, hooks[4], fetch_w0[0][0])
    fetch_w0[1][0]()
    hooks[5][0]()

    def arrived():
        for fetch in fetch_w0:
            fetch[1]()

    hooks[6][0] = arrived
    with jax.named_scope("P10"):
        state_grad(dgu1, w_v, x, dh_v, t_v, dx, None, hooks[6])
    with jax.named_scope("ending"):
        for step in sorted(hooks[7]):
            hooks[7][step]()


def backward(*args):
    n = len(SCATTERS)
    twins = (2, len(SHARES))
    sums = [shaped(2, HIGH * ROWS, D), shaped(2, PAIR, FF), shaped(2, PAIR, FF)]
    outs = [(shaped(T, D), ANY), (shaped(2, 2, T // 2, FF), ANY)] + [(t, VM) for t in sums]
    vmem = [(FF, D), (D, T), (T, D), (2, D, FF), (len(sums), *CUBE, UNITS, PAIR, LANES)]
    scratch = [
        *(pltpu.VMEM(t, BF) for t in vmem),
        *(buf for group in scatter_scratch(n) for buf in group),
        pltpu.SemaphoreType.DMA((n + 1,)),
        pltpu.SemaphoreType.DMA((2, 2, 2)),
        *(pltpu.SemaphoreType.DMA(t) for t in ((*twins, 5), (*twins, 4), (n, len(SHARES)))),
    ]
    return calls(backward_kernel, 1, [ANY] * len(args), outs, scratch)(*args)


def solution(mesh):
    def step(x, dy, wg, wu, wd):
        x, dy = x[0], dy[0]
        gu, down, aT0, ways, act1, h1, aT1, act2, dgu2 = forward(wg, wu, wd, x, dy)
        gu, down = gu.reshape(-1, 2, D, FF), down.reshape(FF, D)
        dx, _, by_d, by_g, by_u = backward(act2, dy, aT1, dgu2, gu, h1, act1, ways, down, aT0, x)
        return dx[None], by_g, by_u, by_d

    seq, rows = P(("rep", "dp"), None, None), P(None, "dp", None)
    return jax.shard_map(
        step, mesh=mesh, in_specs=(seq, seq, rows, rows, rows), out_specs=(seq, *[P("rep", "dp", None)] * 3), check_vma=False
    )
```

profile of v0, /device:TPU:0, one launch (start us, length us, event | category | flops | bytes accessed | tf_op | source)
XLA Modules:
  0.0 301.6 jit_solution(15135541988705857145)
XLA Ops:
  0.6 119.5 %forward_kernel.1 = (bf16[2,2,4,4,4,16,2560]{6,5,4,3,2,1,0:T(8,128)(2,1)}, bf16[4,4,4,5,8,1024]{5,4,3,2,1,0:T(8,128)(2,1)}, bf16[1024,2048]{1,0:T(8,128)(2,1)}, ...) custom-call(bf16[2,16,2560]{2,1,0:T(8,128)(2,1)} %g_ref.1, ...), custom_call_target="tpu_custom_call" | custom-call | tf_op jit(solution)/shard_map/forward_kernel/pallas_call | solution.py:502
  120.1 174.7 %backward_kernel.1 = (bf16[2048,1024]{1,0:T(8,128)(2,1)}, bf16[2,2,1024,2560]{3,2,1,0:T(8,128)(2,1)}, bf16[2,40,1024]{2,1,0:T(8,128)(2,1)}, bf16[2,16,2560]{2,1,0:T(8,128)(2,1)}, bf16[2,16,2560]{2,1,0:T(8,128)(2,1)}) custom-call(bf16[2048,2560]{1,0:T(8,128)(2,1)} %get-tuple-element.17.act2, bf16[2048,1024]{1,0:T(8,128)(2,1)} %bitcast.10, ...), custom_call_target="tpu_custom_call" | custom-call | tf_op jit(solution)/shard_map/backward_kernel/pallas_call | solution.py:739
  294.8 0.0 copy-start.2
  294.8 0.0 copy-start.1
  294.9 0.0 copy-start
  294.9 4.7 %copy.13 = bf16[1,2048,1024]{2,1,0:T(8,128)(2,1)} copy(bf16[1,2048,1024]{2,1,0:T(8,128)(2,1)} %bitcast.12) | data formatting | bytes 8388608
  299.6 0.0 copy-done.2
  299.6 0.7 copy.14
  300.2 0.0 copy-done.1
  300.2 0.7 copy.15
  300.9 0.0 copy-done
  300.9 0.7 copy.16
Async XLA Ops:
  294.8 4.7 %copy-start.2 = (bf16[2,16,2560]{2,1,0:T(8,128)(2,1)S(1)}, bf16[2,16,2560]{2,1,0:T(8,128)(2,1)}, u32[]{:S(2)}) copy-start(bf16[2,16,2560]{2,1,0:T(8,128)(2,1)} %get-tuple-element.35) | copy-start | bytes 491524
  294.8 5.4 %copy-start.1 = (bf16[2,16,2560]{2,1,0:T(8,128)(2,1)S(1)}, bf16[2,16,2560]{2,1,0:T(8,128)(2,1)}, u32[]{:S(2)}) copy-start(bf16[2,16,2560]{2,1,0:T(8,128)(2,1)} %get-tuple-element.36) | copy-start | bytes 491524
  294.9 6.0 %copy-start = (bf16[2,40,1024]{2,1,0:T(8,128)(2,1)S(1)}, bf16[2,40,1024]{2,1,0:T(8,128)(2,1)}, u32[]{:S(2)}) copy-start(bf16[2,40,1024]{2,1,0:T(8,128)(2,1)} %get-tuple-element.37) | copy-start | bytes 491524
where the time goes:
time: 302 us
  Pallas kernels  294 us (97%)
  local copies, waits for them, and re-layouts  6.71 us (2%)
    pallas_call x1, Pallas kernels, backward(): return calls(backward_kernel, 1, [ANY] * len(args), outs, scratch)(*args)  175 us
    pallas_call x1, Pallas kernels, forward(): return call(wg, wu, wd.reshape(layers, HIGH, ROWS, D), x, dy)  119 us
    unnamed x10, local copies, waits for them, and re-layouts  6.71 us

commit v1 on v0

--- a/solution.py
+++ b/solution.py
@@ -370,13 +370,20 @@
     fetch_x, fetch_dy = copy(x_ref, h_v), copy(dy_ref, dy_v)
     puts = [copy(t_v, aT0), copy(t_v, aT1), copy(gu_v.at[0], gu_out.at[0]), copy(gu_v.at[1], gu_out.at[1]), copy(d_v.at[0], d_out)]
     put_t0, put_t1, *put_w = puts
-    fetch_x[0]()
+    entered = enter(place, 1)
     columns, rows_of_down = gather_parts(core)
     half = rows_of_down[0][-1]
-    for n in range(g_ref.shape[0]):
-        gu_v[(n, core, *place.at)] = jnp.where(core == 0, g_ref[n], u_ref[n])
-        d_v[(n, *place.at, EVERY, EVERY, half)] = d_ref[n, :, :, half]
-    entered = enter(place, 1)
+    own = []
+    for n in BOTH:
+        of_down = (EVERY, EVERY, half)
+        own.append(pltpu.make_async_copy(d_ref.at[(n, *of_down)], d_v.at[(n, *place.at, *of_down)], sems.pop()))
+        own[-1].start()
+        at = sems.pop()
+        of_mine = [pltpu.make_async_copy(ref.at[n], gu_v.at[(n, core, *place.at)], at) for ref in (g_ref, u_ref)]
+        for m, fetch in enumerate(of_mine):
+            pl.when(core == m)(fetch.start)
+        own.append(of_mine[0])
+    fetch_x[0]()
     fetch_dy[0]()
     plan = [(gu_v.at[0, core], piece) for piece in columns[0]]
     early, late = columns[1]
@@ -384,6 +391,8 @@
     jobs = [Gather(f"ag{n}", place, *what, send.at[n], recv.at[n]) for n, what in enumerate(plan)]
     prelude, *hooks = spread(jobs, GATHERS, FORWARD_STEPS)
     with jax.named_scope("enter"):
+        for fetch in own:
+            fetch.wait()
         entered()
 
     def norm_rows(k):
@@ -496,9 +505,9 @@
         shaped(T, D), shaped(D, T), shaped(T, FF), shaped(2, T, FF),
     ]
     scratch = [(layers, 2, *CUBE, rows, FF), (layers, *CUBE, HIGH, ROWS, D), (T, D), (T, D), (D, T), (T, D)]
-    sems = [(len(GATHERS),)] + [(len(GATHERS), len(SHARES), 6)] * 2
+    sems = [(11,)] + [(len(GATHERS), len(SHARES), 6)] * 2
     scratch = [pltpu.VMEM(t, BF) for t in scratch] + [pltpu.SemaphoreType.DMA(t) for t in sems]
-    call = calls(forward_kernel, 0, [VM] * 3 + [ANY] * 2, [(t, ANY) for t in outs], scratch)
+    call = calls(forward_kernel, 0, [ANY] * 5, [(t, ANY) for t in outs], scratch)
     return call(wg, wu, wd.reshape(layers, HIGH, ROWS, D), x, dy)
 
 
@@ -690,9 +699,9 @@
             n = len(jobs)
             jobs.append(Scatter(place, mine.at[k], put, n, groups, send, recv, recv_c))
     hooks = spread(jobs, SCATTERS, BACKWARD_STEPS)
-    for phase, step, fetch in ((0, 1, fetch_t), (1, 2, fetch_w), (3, 2, fetch_t0), (3, 0, fetch_d)):
+    for phase, step, fetch in ((0, 1, fetch_t), (0, 2, fetch_w), (3, 2, fetch_t0), (3, 0, fetch_d)):
         hooks[phase][step] = fetch[0]
-    fetch_dy[1]()
+    hooks[0][0] = fetch_dy[1]
     with jax.named_scope("P4"):
         down_grad(act2, dy_v, mine.at[0], hooks[0])
     entered()

time: 302 us -> 299 us (0.990)
  no operation moved by 1% of the time
where the time goes in v1:
time: 299 us
  Pallas kernels  292 us (98%)
  local copies, waits for them, and re-layouts  6.71 us (2%)
    pallas_call x1, Pallas kernels, backward(): return calls(backward_kernel, 1, [ANY] * len(args), outs, scratch)(*args)  173 us
    pallas_call x1, Pallas kernels, forward(): return call(wg, wu, wd.reshape(layers, HIGH, ROWS, D), x, dy)  118 us
    unnamed x10, local copies, waits for them, and re-layouts  6.71 us

profile of v1, /device:TPU:0, one launch (start us, length us, event | category | flops | bytes accessed | tf_op | source)
XLA Modules:
  0.0 298.9 jit_solution(1737404304329107745)
XLA Ops:
  0.6 118.4 %forward_kernel.1 = (bf16[2,2,4,4,4,16,2560]{6,5,4,3,2,1,0:T(8,128)(2,1)}, bf16[4,4,4,5,8,1024]{5,4,3,2,1,0:T(8,128)(2,1)}, bf16[1024,2048]{1,0:T(8,128)(2,1)}, ...) custom-call(bf16[2,16,2560]{2,1,0:T(8,128)(2,1)} %g_ref.1, ...), custom_call_target="tpu_custom_call" | custom-call | tf_op jit(solution)/shard_map/forward_kernel/pallas_call | solution.py:511
  119.0 173.2 %backward_kernel.1 = (bf16[2048,1024]{1,0:T(8,128)(2,1)}, bf16[2,2,1024,2560]{3,2,1,0:T(8,128)(2,1)}, bf16[2,40,1024]{2,1,0:T(8,128)(2,1)}, bf16[2,16,2560]{2,1,0:T(8,128)(2,1)}, bf16[2,16,2560]{2,1,0:T(8,128)(2,1)}) custom-call(bf16[2048,2560]{1,0:T(8,128)(2,1)} %get-tuple-element.17.act2, bf16[2048,1024]{1,0:T(8,128)(2,1)} %bitcast.10, ...), custom_call_target="tpu_custom_call" | custom-call | tf_op jit(solution)/shard_map/backward_kernel/pallas_call | solution.py:748
  292.2 0.0 copy-start.2
  292.2 0.0 copy-start.1
  292.2 0.0 copy-start
  292.2 4.7 %copy.13 = bf16[1,2048,1024]{2,1,0:T(8,128)(2,1)} copy(bf16[1,2048,1024]{2,1,0:T(8,128)(2,1)} %bitcast.12) | data formatting | bytes 8388608
  296.9 0.0 copy-done.2
  296.9 0.7 copy.14
  297.6 0.0 copy-done.1
  297.6 0.7 copy.15
  298.3 0.0 copy-done
  298.3 0.7 copy.16
Async XLA Ops:
  292.2 4.7 %copy-start.2 = (bf16[2,16,2560]{2,1,0:T(8,128)(2,1)S(1)}, bf16[2,16,2560]{2,1,0:T(8,128)(2,1)}, u32[]{:S(2)}) copy-start(bf16[2,16,2560]{2,1,0:T(8,128)(2,1)} %get-tuple-element.35) | copy-start | bytes 491524
  292.2 5.4 %copy-start.1 = (bf16[2,16,2560]{2,1,0:T(8,128)(2,1)S(1)}, bf16[2,16,2560]{2,1,0:T(8,128)(2,1)}, u32[]{:S(2)}) copy-start(bf16[2,16,2560]{2,1,0:T(8,128)(2,1)} %get-tuple-element.36) | copy-start | bytes 491524
  292.2 6.0 %copy-start = (bf16[2,40,1024]{2,1,0:T(8,128)(2,1)S(1)}, bf16[2,40,1024]{2,1,0:T(8,128)(2,1)}, u32[]{:S(2)}) copy-start(bf16[2,40,1024]{2,1,0:T(8,128)(2,1)} %get-tuple-element.37) | copy-start | bytes 491524
